TPU v7x, 32 devices: a whole 2x2x4 slice. The times are simulated.
32 devices in a mesh: dp: 8 (over z, core), expert: 4 (over y, x).
Axes of the slice: x: 2, y: 2, z: 4, core: 2. Of those that a mesh axis runs over, the one named last changes fastest.
Arguments:
- mamba_in: bfloat16 [8, 256, 4096], P('dp'), may hold values from -6 to 6
- conv_state: bfloat16 [8, 3, 8192], P('dp', None, 'expert'), may hold values from -6 to 6
- in_weight: bfloat16 [4096, 8192], P('dp', 'expert'), may hold values from -0.09375 to 0.09375
- conv_kernel: float32 [4, 8192], P(None, 'expert'), may hold values from -3 to 3
- conv_bias: float32 [8192], P('expert'), may hold values from -1 to 1
- moe_in: bfloat16 [512, 4096], P('expert'), may hold values from -6 to 6
- router: bfloat16 [4096, 4], replicated, may hold values from -0.09375 to 0.09375
- expert_ids: int32 [512, 2], P('expert'), may hold values from 0 to 3, all different within a row; in each aligned block of 128 rows (0 to 127, 128 to 255, ...) at most 128 rows name the same one
- w_gate: bfloat16 [4, 4096, 12288], P('expert', None, 'dp'), may hold values from -0.09375 to 0.09375
- w_up: bfloat16 [4, 4096, 12288], P('expert', None, 'dp'), may hold values from -0.09375 to 0.09375
- w_down: bfloat16 [4, 12288, 4096], P('expert', 'dp'), may hold values from -0.078125 to 0.078125
Outputs:
- conv_out: bfloat16 [8, 256, 8192], P('dp', None, 'expert')
- moe_out: bfloat16 [512, 4096], P('expert', 'dp')
Inputs may be any that keep to these rules, and one draw needn't show every extreme that they name: `expert_ids`: each row names two different experts; among the 128 rows of one index of expert no expert is named more than 128 times, a bound that some block reaches.
All inputs are finite; a program needn't handle non-finite values.
Results may differ from a plain program's by a relative error of at most 0.0049.
Values may be sent and summed in bfloat16 or wider, within the bound.
No kernel may reach another device: no remote copies, remote signals or barrier semaphores. Data moves between devices by JAX's collectives and lax.ppermute only.
A program may use at most 192 MiB of HBM per device.

v0:
```python
import jax
import jax.numpy as jnp
from jax import lax
from jax.sharding import PartitionSpec as P


def expert_ffn(inputs, gate_mat, up_mat, down_mat):
    gate_val = jnp.dot(inputs, gate_mat, preferred_element_type=jnp.float32)
    up_val = jnp.dot(inputs, up_mat, preferred_element_type=jnp.float32)
    hidden = (jax.nn.silu(gate_val) * up_val).astype(jnp.bfloat16)
    return jnp.dot(hidden, down_mat, preferred_element_type=jnp.float32)


def body(
    mamba_in,
    conv_state,
    in_weight,
    conv_kernel,
    conv_bias,
    moe_in,
    router,
    expert_ids,
    w_gate,
    w_up,
    w_down,
):
    token_count = mamba_in.shape[1]
    width = mamba_in.shape[2]
    window = mamba_in.reshape(token_count, width)
    channels = in_weight.shape[1]
    taps = conv_kernel.shape[0]
    summed_proj = jnp.dot(
        window,
        lax.all_gather(in_weight, "dp", axis=0, tiled=True),
        preferred_element_type=jnp.float32,
    )
    projected = summed_proj.astype(jnp.bfloat16)
    extended = jnp.concatenate([conv_state[0], projected], axis=0)
    summed = jnp.zeros((token_count, channels), jnp.float32) + conv_bias[None, :]
    for offset in range(taps):
        summed = (
            summed
            + extended[offset : offset + token_count].astype(jnp.float32)
            * conv_kernel[offset][None, :]
        )
    conv_out = jax.nn.silu(summed).astype(jnp.bfloat16).reshape(1, token_count, channels)
    moe_rows = moe_in.shape[0]
    experts = lax.axis_size("expert") * w_gate.shape[0]
    capacity = min(moe_rows, 4 * moe_rows // experts)
    expert_range = jnp.arange(experts, dtype=jnp.int32)
    onehot_ids = (expert_ids.reshape(-1)[:, None] == expert_range[None, :]).astype(jnp.int32)
    earlier = jnp.cumsum(onehot_ids, axis=0) - onehot_ids
    slots = jnp.sum(earlier * onehot_ids, axis=1).reshape(moe_rows, 2)
    targets = expert_ids * capacity + slots
    slot_range = jnp.arange(experts * capacity, dtype=jnp.int32)
    first_hit = targets[:, 0][None, :] == slot_range[:, None]
    second_hit = targets[:, 1][None, :] == slot_range[:, None]
    dispatch_table = jnp.logical_or(first_hit, second_hit).astype(jnp.bfloat16)
    send_buffer = jnp.dot(dispatch_table, moe_in, preferred_element_type=jnp.float32).astype(
        jnp.bfloat16
    )
    send_buffer = send_buffer.reshape(experts, capacity, width)
    logits = jnp.dot(moe_in, router, preferred_element_type=jnp.float32)
    chosen_mask = (expert_ids[:, :, None] == expert_range[None, None, :]).astype(jnp.float32)
    chosen = jnp.sum(logits[:, None, :] * chosen_mask, axis=2)
    first_weight = jax.nn.sigmoid(chosen[:, 0] - chosen[:, 1])
    combine_table = first_weight[:, None] * first_hit.T.astype(jnp.float32) + (1.0 - first_weight)[
        :, None
    ] * second_hit.T.astype(jnp.float32)
    received = lax.all_to_all(send_buffer, "expert", split_axis=0, concat_axis=0, tiled=True)
    flat_rows = received.reshape(-1, width)
    result = expert_ffn(flat_rows, w_gate[0], w_up[0], w_down[0])
    partials = result.reshape(received.shape[0], received.shape[1], width)
    shares = lax.psum_scatter(partials, "dp", scatter_dimension=2, tiled=True)
    returned = lax.all_to_all(shares, "expert", split_axis=0, concat_axis=0, tiled=True)
    flat_back = returned.reshape(experts * capacity, returned.shape[2])
    mixed = jnp.dot(
        combine_table,
        flat_back,
        precision=lax.Precision.HIGHEST,
        preferred_element_type=jnp.float32,
    )
    return (conv_out, mixed.astype(jnp.bfloat16))


def solution(mesh):
    in_specs = (
        P("dp", None, None),
        P("dp", None, "expert"),
        P("dp", "expert"),
        P(None, "expert"),
        P("expert"),
        P("expert", None),
        P(),
        P("expert", None),
        P("expert", None, "dp"),
        P("expert", None, "dp"),
        P("expert", "dp", None),
    )
    out_specs = (P("dp", None, "expert"), P("expert", "dp"))
    return jax.shard_map(body, mesh=mesh, in_specs=in_specs, out_specs=out_specs, check_vma=False)
```

profile of v0, /device:TPU:0, one launch (start us, length us, event | category | flops | bytes accessed | tf_op | source)
XLA Modules:
  0.0 353.5 jit_solution(8871153900584539604)
XLA Ops:
  7.2 0.0 copy-start
  7.2 0.0 reduce-scatter.2.cloned.1.call-start
  7.2 0.9 copy.39
  8.2 0.1 eq.86
  8.3 0.1 eq.82
  8.4 1.2 reduce-window.6
  9.7 0.1 slice.56
  9.7 0.1 copy.41
  9.9 0.1 copy.42
  10.0 0.1 add_bitcast_fusion
  10.1 0.1 reshape.49
  10.2 0.1 copy.43
  10.3 0.7 multiply_add_fusion
  11.0 0.0 copy-start.6
  11.0 2.6 convolution_convert_fusion
  13.6 0.0 slice-start
  13.6 53.1 %all_to_all.10 = bf16[4,128,4096]{2,1,0:T(8,128)(2,1)S(1)} all-to-all(bf16[4,128,4096]{2,1,0:T(8,128)(2,1)S(1)} %bitcast.62), channel_id=1, replica_groups=mesh['dp'=8,'expert'=4] {'expert'}, dimensions={0} | all-to-all | bytes 8388608 | tf_op jit(solution)/shard_map/all_to_all | solution.py:70
  66.7 0.0 copy-done.6
  66.7 0.0 slice-start.1
  66.7 0.0 slice-start.2
  66.7 8.3 %fusion.4 = f32[512,1536]{1,0:T(8,128)} fusion(bf16[512,4096]{1,0:T(8,128)(2,1)S(1)} %bitcast.63, bf16[1,4096,1536]{2,1,0:T(8,128)(2,1)S(1)} %copy-done.6), kind=kOutput, calls=%fused_computation.4 | convolution fusion | flops 6442450944 | bytes 19922944 | tf_op jit(solution)/shard_map/dot_general | solution.py:8
  75.0 0.0 slice-done
  75.0 0.0 slice-done.1
  75.0 0.0 slice-done.2
  75.0 8.5 %fusion.9 = bf16[512,1536]{1,0:T(8,128)(2,1)S(1)} fusion(bf16[512,4096]{1,0:T(8,128)(2,1)S(1)} %bitcast.64, bf16[1,4096,1536]{2,1,0:T(8,128)(2,1)S(1)} %bitcast.74, f32[512,1536]{1,0:T(8,128)} %fusion.4), kind=kOutput, calls=%fused_computation.8 | convolution fusion | flops 6447169536 | bytes 21495808 | tf_op jit(solution)/shard_map/dot_general | solution.py:9
  83.5 11.8 %fusion = f32[4,128,4096]{2,1,0:T(8,128)} fusion(bf16[4,128,1536]{2,1,0:T(8,128)(2,1)S(1)} %bitcast.75, bf16[1,1536,4096]{2,1,0:T(8,128)(2,1)} %param.21), kind=kOutput, calls=%fused_computation | convolution fusion | flops 6442450944 | bytes 22544384 | tf_op jit(solution)/shard_map/dot_general | solution.py:11
  95.3 0.0 reduce-scatter.2.cloned.1.call-update
  95.4 0.0 copy-start.1
  95.4 0.0 all-gather.2.cloned.1.call-start
  95.4 0.7 all-gather.2.cloned.1.call-update
  96.1 0.0 copy-start.4
  96.1 0.0 copy-start.2
  96.2 88.7 %reduce-scatter.2.cloned.1.call-done = f32[4,128,512]{2,1,0:T(8,128)} async-done(((f32[4,128,4096]{2,1,0:T(8,128)}), f32[4,128,512]{2,1,0:T(8,128)}) %reduce-scatter.2.cloned.1.call-update) | async-done | bytes 1048592 | tf_op jit(solution)/shard_map/reduce_scatter | solution.py:74
  184.8 3.7 %all-to-all-start.1 = ((f32[4,128,512]{2,1,0:T(8,128)}), f32[4,128,512]{2,1,0:T(8,128)S(1)}, u32[]{:S(2)}, u32[]{:S(2)}) async-start(f32[4,128,512]{2,1,0:T(8,128)} %reduce-scatter.2.cloned.1.call-done), calls=%async_computation.2 | async-start | bytes 2097152 | tf_op jit(solution)/shard_map/all_to_all | solution.py:75
  188.5 0.0 copy-done.1
  188.6 1.6 fusion.33
  190.2 0.0 copy-done.4
  190.2 0.0 copy-done.2
  190.2 9.9 %all-to-all-done.1 = f32[4,128,512]{2,1,0:T(8,128)S(1)} async-done(((f32[4,128,512]{2,1,0:T(8,128)}), f32[4,128,512]{2,1,0:T(8,128)S(1)}, u32[]{:S(2)}, u32[]{:S(2)}) %all-to-all-start.1) | async-done | bytes 1048608 | tf_op jit(solution)/shard_map/all_to_all | solution.py:75
  200.1 1.4 convolution_convert_fusion.2
  201.5 0.0 copy-start.3
  201.5 0.0 copy-start.5
  201.5 134.5 %all-gather.2.cloned.1.call-done = bf16[4096,2048]{1,0:T(8,128)(2,1)} async-done(((bf16[512,2048]{1,0:T(8,128)(2,1)}), bf16[4096,2048]{1,0:T(8,128)(2,1)}) %all-gather.2.cloned.1.call-update) | async-done | bytes 16777232 | tf_op jit(solution)/shard_map/all_gather | solution.py:34
  336.0 0.0 copy-done
  336.0 8.3 %convolution_convert_fusion.1 = bf16[256,2048]{1,0:T(8,128)(2,1)S(1)} fusion(bf16[4096,2048]{1,0:T(8,128)(2,1)} %all-gather.2.cloned.1.call-done, bf16[1,256,4096]{2,1,0:T(8,128)(2,1)S(1)} %copy-done), kind=kOutput, calls=%fused_computation.9 | convolution fusion | flops 4295491584 | bytes 19922944 | tf_op jit(solution)/shard_map/dot_general | solution.py:32
  344.3 0.0 copy-done.3
  344.3 0.0 copy-done.5
  344.3 2.3 fusion.15
  (9 shorter events, 0.1 us)
Async XLA Ops:
  7.2 328.8 %copy-start = (bf16[1,256,4096]{2,1,0:T(8,128)(2,1)S(1)}, bf16[1,256,4096]{2,1,0:T(8,128)(2,1)}, u32[]{:S(2)}) copy-start(bf16[1,256,4096]{2,1,0:T(8,128)(2,1)} %param.11) | copy-start | bytes 6291460
  7.2 177.7 %reduce-scatter.2.cloned.1.call-start = ((), (), s32[]{:S(2)}) async-start(), calls=%async_computation.4 | async-start | bytes 9437184 | tf_op jit(solution)/shard_map/reduce_scatter | solution.py:74
  11.0 55.7 %copy-start.6 = (bf16[1,4096,1536]{2,1,0:T(8,128)(2,1)S(1)}, bf16[1,4096,1536]{2,1,0:T(8,128)(2,1)}, u32[]{:S(2)}) copy-start(bf16[1,4096,1536]{2,1,0:T(8,128)(2,1)} %param.19) | copy-start | bytes 37748740
  13.6 61.4 %slice-start = ((s8[12582912]{0:T(1024)(128)(4,1)}), s8[4194304]{0:T(1024)(128)(4,1)S(1)}, s32[]{:S(2)}) async-start(s8[12582912]{0:T(1024)(128)(4,1)} %bitcast.73), calls=%async_computation.5 | async-start | bytes 8388608
  66.7 8.3 %slice-start.1 = ((s8[12582912]{0:T(1024)(128)(4,1)}), s8[4194304]{0:T(1024)(128)(4,1)S(1)}, s32[]{:S(2)}) async-start(s8[12582912]{0:T(1024)(128)(4,1)} %bitcast.73), calls=%async_computation.6 | async-start | bytes 8388608
  66.7 8.3 %slice-start.2 = ((s8[12582912]{0:T(1024)(128)(4,1)}), s8[4194304]{0:T(1024)(128)(4,1)S(1)}, s32[]{:S(2)}) async-start(s8[12582912]{0:T(1024)(128)(4,1)} %bitcast.73), calls=%async_computation.7 | async-start | bytes 8388608
  95.4 93.2 %copy-start.1 = (bf16[4096,4]{0,1:T(4,128)(2,1)S(1)}, bf16[4096,4]{0,1:T(4,128)(2,1)}, u32[]{:S(2)}) copy-start(bf16[4096,4]{0,1:T(4,128)(2,1)} %param.17) | copy-start | bytes 98308
  95.4 240.6 %all-gather.2.cloned.1.call-start = ((), (), s32[]{:S(2)}) async-start(), calls=%async_computation.3 | async-start | bytes 18874368 | tf_op jit(solution)/shard_map/all_gather | solution.py:34
  96.1 94.0 %copy-start.4 = (s32[128,2]{0,1:T(2,128)S(1)}, s32[128,2]{0,1:T(2,128)}, u32[]{:S(2)}) copy-start(s32[128,2]{0,1:T(2,128)} %param.18) | copy-start | bytes 3076
  96.1 94.1 %copy-start.2 = (f32[4,2048]{1,0:T(4,128)S(1)}, f32[4,2048]{1,0:T(4,128)}, u32[]{:S(2)}) copy-start(f32[4,2048]{1,0:T(4,128)} %param.14) | copy-start | bytes 98308
  184.8 15.3 %all-to-all-start.1 = ((f32[4,128,512]{2,1,0:T(8,128)}), f32[4,128,512]{2,1,0:T(8,128)S(1)}, u32[]{:S(2)}, u32[]{:S(2)}) async-start(f32[4,128,512]{2,1,0:T(8,128)} %reduce-scatter.2.cloned.1.call-done), calls=%async_computation.2 | async-start | bytes 2097152 | tf_op jit(solution)/shard_map/all_to_all | solution.py:75
  201.5 142.7 %copy-start.3 = (bf16[1,3,2048]{2,1,0:T(4,128)(2,1)S(1)}, bf16[1,3,2048]{2,1,0:T(4,128)(2,1)}, u32[]{:S(2)}) copy-start(bf16[1,3,2048]{2,1,0:T(4,128)(2,1)} %param.12) | copy-start | bytes 36868
  201.5 142.7 %copy-start.5 = (f32[2048]{0:T(1024)S(1)}, f32[2048]{0:T(1024)}, u32[]{:S(2)}) copy-start(f32[2048]{0:T(1024)} %param.15) | copy-start | bytes 24580
Sparse Core Ops, SparseCore 0:
  95.5 89.3 reduce-scatter.1
  186.4 149.5 all-gather.1
where the time goes:
time: 354 us; the launch traced here: 353 us
  waiting for transfers between devices  234 us (66%)
  blocking collectives  53.1 us (15%)
  matrix products  42.5 us (12%)
  between operations  14.2 us (4%)
  other arithmetic  4.44 us (1%)
  starting transfers between devices  3.77 us (1%)
    all_gather x1, waiting for transfers between devices, body(): lax.all_gather(in_weight, 'dp', axis=0, tiled=True)  134 us
    reduce_scatter x1, waiting for transfers between devices, body(): shares = lax.psum_scatter(partials, 'dp', scatter_dimension=2, tiled=True)  88.7 us
    all_to_all x1, blocking collectives, body(): lax.all_to_all(send_buffer, 'expert', split_axis=0, concat_axis=0, tiled=...  53.1 us
    dot_general x1, matrix products, expert_ffn(): return jnp.dot(hidden, down_mat, preferred_element_type=jnp.float32)  11.8 us
    all_to_all x1, waiting for transfers between devices, body(): lax.all_to_all(shares, 'expert', split_axis=0, concat_axis=0, tiled=True)  9.86 us
    dot_general x1, matrix products, expert_ffn(): up_val = jnp.dot(inputs, up_mat, preferred_element_type=jnp.float32)  8.53 us
    dot_general x1, matrix products, expert_ffn(): gate_val = jnp.dot(inputs, gate_mat, preferred_element_type=jnp.float32)  8.28 us
    dot_general x1, matrix products, body(): jnp.dot(window, lax.all_gather(in_weight, 'dp', axis=0, tiled=True), pref...  8.25 us
  transfers between devices with their start and end apart: 3, of which 3 were waited for; matrix products, arithmetic and copies ran while one was open for 1% of the time, Pallas kernels for 0%

commit v1 on v0

--- a/solution.py
+++ b/solution.py
@@ -2,6 +2,18 @@
 import jax.numpy as jnp
 from jax import lax
 from jax.sharding import PartitionSpec as P
+
+
+def in_blocks(x, dim, length):
+    lengths = x.shape
+    blocks = x.reshape(*lengths[:dim], length, lengths[dim] // length, *lengths[dim + 1 :])
+    return jnp.moveaxis(blocks, dim, 0)
+
+
+def in_order(pieces, dim):
+    pieces = jnp.moveaxis(pieces, 0, dim)
+    shape = pieces.shape
+    return pieces.reshape(*shape[:dim], shape[dim] * shape[dim + 1], *shape[dim + 2 :])
 
 
 def expert_ffn(inputs, gate_mat, up_mat, down_mat):
@@ -72,7 +84,14 @@
     result = expert_ffn(flat_rows, w_gate[0], w_up[0], w_down[0])
     partials = result.reshape(received.shape[0], received.shape[1], width)
     shares = lax.psum_scatter(partials, "dp", scatter_dimension=2, tiled=True)
-    returned = lax.all_to_all(shares, "expert", split_axis=0, concat_axis=0, tiled=True)
+    size, index = (lax.axis_size("expert"), lax.axis_index("expert"))
+    parts = in_blocks(shares, 0, size)
+    finished = [parts[index]]
+    for step in range(1, size):
+        sent = parts[index ^ step]
+        finished.append(lax.ppermute(sent, "expert", [(i, i ^ step) for i in range(size)]))
+    parts = jnp.stack(finished)[index ^ jnp.arange(size)]
+    returned = in_order(parts, 0)
     flat_back = returned.reshape(experts * capacity, returned.shape[2])
     mixed = jnp.dot(
         combine_table,

time: 354 us -> 353 us (level)
  waiting for transfers between devices: 234 us -> 230 us
    all_to_all x1 -> x0, waiting for transfers between devices: 9.86 us -> none  [body(): lax.all_to_all(shares, 'expert', split_axis=0, concat_axis=0, tiled=True)]
    ppermute x0 -> x3, waiting for transfers between devices: none -> 8.97 us  [body(): lax.ppermute(sent, 'expert', [(i, i ^ step) for i in range(size)])]
    all_to_all x1 -> x0, starting transfers between devices: 3.7 us -> none  [body(): lax.all_to_all(shares, 'expert', split_axis=0, concat_axis=0, tiled=True)]
    ppermute x0 -> x3, starting transfers between devices: none -> 3.55 us  [body(): lax.ppermute(sent, 'expert', [(i, i ^ step) for i in range(size)])]
  transfers between devices with their start and end apart: 3 -> 5, of which waited for: 3 -> 4; matrix products, arithmetic and copies ran while one was open for 1% -> 2% of each run, Pallas kernels for 0% -> 0%
where the time goes in v1:
time: 353 us
  waiting for transfers between devices  230 us (65%)
  blocking collectives  53.1 us (15%)
  matrix products  40.4 us (11%)
  between operations  14.2 us (4%)
  other arithmetic  5.49 us (2%)
  local copies, waits for them, and re-layouts  5.25 us (1%)
  starting transfers between devices  3.81 us (1%)
    all_gather x1, waiting for transfers between devices, body(): lax.all_gather(in_weight, 'dp', axis=0, tiled=True)  133 us
    reduce_scatter x1, waiting for transfers between devices, body(): shares = lax.psum_scatter(partials, 'dp', scatter_dimension=2, tiled=True)  87.8 us
    all_to_all x1, blocking collectives, body(): lax.all_to_all(send_buffer, 'expert', split_axis=0, concat_axis=0, tiled=...  53.1 us
    dot_general x1, matrix products, expert_ffn(): up_val = jnp.dot(inputs, up_mat, preferred_element_type=jnp.float32)  10.4 us
    ppermute x3, waiting for transfers between devices, body(): lax.ppermute(sent, 'expert', [(i, i ^ step) for i in range(size)])  8.97 us
    dot_general x1, matrix products, expert_ffn(): return jnp.dot(hidden, down_mat, preferred_element_type=jnp.float32)  8.92 us
    dot_general x1, matrix products, expert_ffn(): gate_val = jnp.dot(inputs, gate_mat, preferred_element_type=jnp.float32)  8.32 us
    dot_general x1, matrix products, body(): jnp.dot(window, lax.all_gather(in_weight, 'dp', axis=0, tiled=True), pref...  8.25 us
  transfers between devices with their start and end apart: 5, of which 4 were waited for; matrix products, arithmetic and copies ran while one was open for 2% of the time, Pallas kernels for 0%

profile of v1, /device:TPU:0, one launch (start us, length us, event | category | flops | bytes accessed | tf_op | source)
XLA Modules:
  0.0 352.5 jit_solution(6554081577197939911)
XLA Ops:
  7.2 0.0 copy-start
  7.2 0.0 reduce-scatter.2.cloned.1.call-start
  7.2 0.9 copy.39
  8.2 0.1 eq.86
  8.3 0.1 eq.82
  8.4 1.2 reduce-window.6
  9.7 0.1 slice.58
  9.7 0.1 copy.41
  9.9 0.1 copy.42
  10.0 0.1 add_bitcast_fusion
  10.1 0.1 reshape.70
  10.2 0.1 copy.43
  10.3 0.7 multiply_add_fusion
  11.0 2.6 convolution_convert_fusion
  13.6 53.1 %all_to_all.5 = bf16[4,128,4096]{2,1,0:T(8,128)(2,1)S(1)} all-to-all(bf16[4,128,4096]{2,1,0:T(8,128)(2,1)S(1)} %bitcast.71), channel_id=1, replica_groups=mesh['dp'=8,'expert'=4] {'expert'}, dimensions={0} | all-to-all | bytes 8388608 | tf_op jit(solution)/shard_map/all_to_all | solution.py:82
  66.7 0.0 copy-done.7
  66.7 8.3 %fusion.4 = f32[512,1536]{1,0:T(8,128)} fusion(bf16[512,4096]{1,0:T(8,128)(2,1)S(1)} %bitcast.73, bf16[1,4096,1536]{2,1,0:T(8,128)(2,1)S(1)} %copy-done.7), kind=kOutput, calls=%fused_computation.5 | convolution fusion | flops 6442450944 | bytes 19922944 | tf_op jit(solution)/shard_map/dot_general | solution.py:20
  75.0 10.4 %fusion.9 = bf16[512,1536]{1,0:T(8,128)(2,1)S(1)} fusion(bf16[512,4096]{1,0:T(8,128)(2,1)S(1)} %bitcast.74, bf16[1,4096,1536]{2,1,0:T(8,128)(2,1)} %param.20, f32[512,1536]{1,0:T(8,128)} %fusion.4), kind=kOutput, calls=%fused_computation.9 | convolution fusion | flops 6447169536 | bytes 21495808 | tf_op jit(solution)/shard_map/dot_general | solution.py:21
  85.5 0.0 slice-done
  85.5 0.0 slice-done.1
  85.5 0.0 slice-done.2
  85.5 8.9 %fusion = f32[4,128,4096]{2,1,0:T(8,128)} fusion(bf16[4,128,1536]{2,1,0:T(8,128)(2,1)S(1)} %bitcast.87, bf16[1,1536,4096]{2,1,0:T(8,128)(2,1)S(1)} %bitcast.86), kind=kOutput, calls=%fused_computation.1 | convolution fusion | flops 6442450944 | bytes 22544384 | tf_op jit(solution)/shard_map/dot_general | solution.py:23
  94.5 0.0 reduce-scatter.2.cloned.1.call-update
  94.5 0.0 copy-start.1
  94.5 0.0 copy-start.2
  94.5 0.0 copy-start.5
  94.5 0.0 copy-start.3
  94.5 0.2 all-gather.2.cloned.1.call-start
  94.8 0.5 all-gather.2.cloned.1.call-update
  95.3 0.4 copy-done.1
  95.7 0.0 copy-done.2
  95.7 0.4 fusion.34
  96.2 87.8 %reduce-scatter.2.cloned.1.call-done = f32[4,128,512]{2,1,0:T(8,128)} async-done(((f32[4,128,4096]{2,1,0:T(8,128)}), f32[4,128,512]{2,1,0:T(8,128)}) %reduce-scatter.2.cloned.1.call-update) | async-done | bytes 1048592 | tf_op jit(solution)/shard_map/reduce_scatter | solution.py:86
  184.0 1.3 dynamic-slice_bitcast_fusion
  185.2 2.4 collective-permute-start.2
  187.7 0.6 collective-permute-start.1
  188.2 0.5 collective-permute-start
  188.8 6.2 %collective-permute-done.2 = f32[1,128,512]{2,1,0:T(8,128)S(1)} collective-permute-done((f32[1,128,512]{2,1,0:T(8,128)S(1)}, f32[1,128,512]{2,1,0:T(8,128)S(1)}, u32[]{:S(2)}, u32[]{:S(2)}) %collective-permute-start.2) | collective-permute-done | bytes 262176 | tf_op jit(solution)/shard_map/ppermute | solution.py:92
  195.0 2.7 collective-permute-done.1
  197.7 0.0 collective-permute-done
  197.8 1.0 maximum_bitcast_fusion
  198.8 1.8 gather_fusion
  200.6 1.4 convolution_convert_fusion.2
  202.1 133.0 %all-gather.2.cloned.1.call-done = bf16[4096,2048]{1,0:T(8,128)(2,1)} async-done(((bf16[512,2048]{1,0:T(8,128)(2,1)}), bf16[4096,2048]{1,0:T(8,128)(2,1)}) %all-gather.2.cloned.1.call-update) | async-done | bytes 16777232 | tf_op jit(solution)/shard_map/all_gather | solution.py:46
  335.1 8.3 %convolution_convert_fusion.1 = bf16[256,2048]{1,0:T(8,128)(2,1)S(1)} fusion(bf16[4096,2048]{1,0:T(8,128)(2,1)} %all-gather.2.cloned.1.call-done, bf16[1,256,4096]{2,1,0:T(8,128)(2,1)S(1)} %copy-done), kind=kOutput, calls=%fused_computation.10 | convolution fusion | flops 4295491584 | bytes 19922944 | tf_op jit(solution)/shard_map/dot_general | solution.py:44
  343.3 0.0 copy-done.4
  343.3 0.0 copy-done.6
  343.4 2.3 fusion.15
  (20 shorter events, 0.2 us)
Async XLA Ops:
  7.2 327.9 %copy-start = (bf16[1,256,4096]{2,1,0:T(8,128)(2,1)S(1)}, bf16[1,256,4096]{2,1,0:T(8,128)(2,1)}, u32[]{:S(2)}) copy-start(bf16[1,256,4096]{2,1,0:T(8,128)(2,1)} %param.11) | copy-start | bytes 6291460
  7.2 176.8 %reduce-scatter.2.cloned.1.call-start = ((), (), s32[]{:S(2)}) async-start(), calls=%async_computation.3 | async-start | bytes 9437184 | tf_op jit(solution)/shard_map/reduce_scatter | solution.py:86
  11.0 55.7 %copy-start.7 = (bf16[1,4096,1536]{2,1,0:T(8,128)(2,1)S(1)}, bf16[1,4096,1536]{2,1,0:T(8,128)(2,1)}, u32[]{:S(2)}) copy-start(bf16[1,4096,1536]{2,1,0:T(8,128)(2,1)} %param.19) | copy-start | bytes 37748740
  66.7 18.8 %slice-start = ((s8[12582912]{0:T(1024)(128)(4,1)}), s8[4194304]{0:T(1024)(128)(4,1)S(1)}, s32[]{:S(2)}) async-start(s8[12582912]{0:T(1024)(128)(4,1)} %bitcast.85), calls=%async_computation.4 | async-start | bytes 8388608
  66.7 18.8 %slice-start.1 = ((s8[12582912]{0:T(1024)(128)(4,1)}), s8[4194304]{0:T(1024)(128)(4,1)S(1)}, s32[]{:S(2)}) async-start(s8[12582912]{0:T(1024)(128)(4,1)} %bitcast.85), calls=%async_computation.5 | async-start | bytes 8388608
  75.0 10.5 %slice-start.2 = ((s8[12582912]{0:T(1024)(128)(4,1)}), s8[4194304]{0:T(1024)(128)(4,1)S(1)}, s32[]{:S(2)}) async-start(s8[12582912]{0:T(1024)(128)(4,1)} %bitcast.85), calls=%async_computation.6 | async-start | bytes 8388608
  94.5 1.2 copy-start.1
  94.5 1.2 copy-start.2
  94.5 1.6 copy-start.5
  94.5 1.6 copy-start.3
  94.5 240.5 %all-gather.2.cloned.1.call-start = ((), (), s32[]{:S(2)}) async-start(), calls=%async_computation.2 | async-start | bytes 18874368 | tf_op jit(solution)/shard_map/all_gather | solution.py:46
  185.2 9.8 %collective-permute-start.2 = (f32[1,128,512]{2,1,0:T(8,128)S(1)}, f32[1,128,512]{2,1,0:T(8,128)S(1)}, u32[]{:S(2)}, u32[]{:S(2)}) collective-permute-start(f32[1,128,512]{2,1,0:T(8,128)S(1)} %get-tuple-element.5), channel_id=1, source_target_pairs={{0,3},{1,2},{2,1},{3,0},{4,7},{5,6},{6,5},{7,4},{8,11},{9,10},{10,... | collective-permute-start | bytes 786440 | tf_op jit(solution)/shard_map/ppermute | solution.py:92
  187.7 10.1 %collective-permute-start.1 = (f32[1,128,512]{2,1,0:T(8,128)S(1)}, f32[1,128,512]{2,1,0:T(8,128)S(1)}, u32[]{:S(2)}, u32[]{:S(2)}) collective-permute-start(f32[1,128,512]{2,1,0:T(8,128)S(1)} %get-tuple-element.6), channel_id=1, source_target_pairs={{0,2},{1,3},{2,0},{3,1},{4,6},{5,7},{6,4},{7,5},{8,10},{9,11},{10,... | collective-permute-start | bytes 786440 | tf_op jit(solution)/shard_map/ppermute | solution.py:92
  188.2 9.5 %collective-permute-start = (f32[1,128,512]{2,1,0:T(8,128)S(1)}, f32[1,128,512]{2,1,0:T(8,128)S(1)}, u32[]{:S(2)}, u32[]{:S(2)}) collective-permute-start(f32[1,128,512]{2,1,0:T(8,128)S(1)} %get-tuple-element.7), channel_id=1, source_target_pairs={{0,1},{1,0},{2,3},{3,2},{4,5},{5,4},{6,7},{7,6},{8,9},{9,8},{10,11... | collective-permute-start | bytes 786440 | tf_op jit(solution)/shard_map/ppermute | solution.py:92
  202.1 141.3 %copy-start.4 = (bf16[1,3,2048]{2,1,0:T(4,128)(2,1)S(1)}, bf16[1,3,2048]{2,1,0:T(4,128)(2,1)}, u32[]{:S(2)}) copy-start(bf16[1,3,2048]{2,1,0:T(4,128)(2,1)} %param.12) | copy-start | bytes 36868
  202.1 141.3 %copy-start.6 = (f32[2048]{0:T(1024)S(1)}, f32[2048]{0:T(1024)}, u32[]{:S(2)}) copy-start(f32[2048]{0:T(1024)} %param.15) | copy-start | bytes 24580
Sparse Core Ops, SparseCore 0:
  94.6 89.3 reduce-scatter.1
  185.6 149.4 all-gather.1
